TPU v7x, 32 devices: a whole 2x2x4 slice. The times are simulated.
32 devices in a mesh: gx: 4 (over z), gy: 8 (over y, x, core).
Axes of the slice: x: 2, y: 2, z: 4, core: 2. Of those that a mesh axis runs over, the one named last changes fastest.
Arguments:
- tables: float32 [2, 262144, 128], P(None, ('gx', 'gy')), may hold values from -0.9 to 0.9
- cold_rows: int32 [32, 2, 32, 16], P(('gx', 'gy')), may hold values from 0 to 8191, as said below
- cold_bags: int32 [32, 2, 32, 16], P(('gx', 'gy')), may hold values from -1 to 127, as said below
- hot_rows: int32 [2, 256], replicated, may hold values from 0 to 262143
- hot_ids: int32 [4096, 2, 8], P(('gx', 'gy')), may hold values from 0 to 255
Outputs:
- pooled: float32 [4096, 2, 128], P(('gx', 'gy'))
Inputs may be any that keep to these rules, and one draw needn't show every extreme that they name: `cold_rows`: every entry names one of the owner's 8192 rows. `cold_bags`: live slots of one sender, table and owner come first, the empty ones (-1) after them; in every draw each table has an owner whose 16 slots are all live from every sender.
All inputs are finite; a program needn't handle non-finite values.
Results may differ from a plain program's by a relative error of at most 0.0003.
Values sent between devices are 32-bit elements; how exact they have to be, the bound alone decides.
No kernel may reach another device: no remote copies, remote signals or barrier semaphores. Data moves between devices by JAX's collectives and lax.ppermute only.
A program may use at most 64 MiB of HBM per device.

v0:
```python
import math
import jax
import jax.numpy as jnp
from jax import lax
from jax.sharding import PartitionSpec as P


def pick_rows(table, indices):
    count = indices.shape[0]
    block = math.gcd(512, count)
    row_ids = jnp.arange(table.shape[0], dtype=jnp.int32)
    grouped = indices.reshape(count // block, block)

    def one_block(wanted):
        selector = (wanted[:, None] == row_ids[None, :]).astype(jnp.float32)
        return jnp.dot(
            selector, table, precision=lax.Precision.HIGHEST, preferred_element_type=jnp.float32
        )

    return lax.map(one_block, grouped).reshape(count, table.shape[1])


def body(tables, cold_rows, cold_bags, hot_rows, hot_ids):
    axis_x = lax.axis_size("gx")
    axis_y = lax.axis_size("gy")
    peer_count = axis_x * axis_y
    table_count, rows_dev, emb_width = tables.shape
    slot_cap = cold_rows.shape[3]
    batch_rows = hot_ids.shape[0]
    hot_count = hot_rows.shape[1]
    my_index = lax.axis_index(("gx", "gy"))
    hot_owner = hot_rows // rows_dev
    local_rows = jnp.where(hot_owner == my_index, hot_rows - my_index * rows_dev, -1)
    picked = jax.vmap(pick_rows)(tables, local_rows)
    hot_table = lax.psum(picked, ("gx", "gy"))
    matches = jnp.sum(
        (
            hot_ids[:, :, :, None] == jnp.arange(hot_count, dtype=jnp.int32)[None, None, None, :]
        ).astype(jnp.float32),
        axis=2,
    )
    hot_part = jnp.einsum("bth,thd->btd", matches, hot_table, precision=lax.Precision.HIGHEST)
    my_rows = cold_rows[0]
    my_bags = cold_bags[0]
    got_rows, got_bags = (
        lax.all_to_all(my_rows, ("gx", "gy"), split_axis=1, concat_axis=1, tiled=True),
        lax.all_to_all(my_bags, ("gx", "gy"), split_axis=1, concat_axis=1, tiled=True),
    )
    wanted_rows = jnp.where(got_bags >= 0, got_rows, -1)
    looked = jax.vmap(pick_rows)(tables, wanted_rows.reshape(table_count, -1))
    looked = looked.reshape(table_count, peer_count, slot_cap, emb_width)
    samples = jnp.arange(batch_rows, dtype=jnp.int32)
    returned = lax.all_to_all(looked, ("gx", "gy"), split_axis=1, concat_axis=1, tiled=True)
    onehot = (my_bags[:, None, :, :] == samples[None, :, None, None]).astype(jnp.float32)
    cold_part = jnp.einsum("tbpc,tpcd->btd", onehot, returned, precision=lax.Precision.HIGHEST)
    return cold_part + hot_part


def solution(mesh):
    return jax.shard_map(
        body,
        mesh=mesh,
        in_specs=(
            P(None, ("gx", "gy"), None),
            P(("gx", "gy"), None, None, None),
            P(("gx", "gy"), None, None, None),
            P(),
            P(("gx", "gy"), None, None),
        ),
        out_specs=P(("gx", "gy"), None, None),
        check_vma=False,
    )
```

profile of v0, /device:TPU:0, one launch (start us, length us, event | category | flops | bytes accessed | tf_op | source)
XLA Modules:
  0.0 203.2 jit_solution(9199264976657592994)
XLA Ops:
  6.5 1.4 copy.23
  7.9 7.3 %all-to-all-start.1 = ((s32[2,32,16]{2,0,1:T(2,128)}), s32[2,32,16]{2,0,1:T(2,128)S(1)}, u32[]{:S(2)}, u32[]{:S(2)}) async-start(s32[2,32,16]{2,0,1:T(2,128)} %bitcast.1), calls=%async_computation.1 | async-start | bytes 65536 | tf_op jit(solution)/shard_map/all_to_all | solution.py:46
  15.3 1.4 copy.22
  16.7 5.9 %all-to-all-done.1 = s32[2,32,16]{2,0,1:T(2,128)S(1)} async-done(((s32[2,32,16]{2,0,1:T(2,128)}), s32[2,32,16]{2,0,1:T(2,128)S(1)}, u32[]{:S(2)}, u32[]{:S(2)}) %all-to-all-start.1) | async-done | bytes 4128 | tf_op jit(solution)/shard_map/all_to_all | solution.py:46
  22.5 2.6 %all-to-all-start = ((s32[2,32,16]{2,0,1:T(2,128)}), s32[2,32,16]{2,0,1:T(2,128)S(1)}, u32[]{:S(2)}, u32[]{:S(2)}) async-start(s32[2,32,16]{2,0,1:T(2,128)} %bitcast), calls=%async_computation | async-start | bytes 65536 | tf_op jit(solution)/shard_map/all_to_all | solution.py:47
  25.1 7.2 %all-to-all-done = s32[2,32,16]{2,0,1:T(2,128)S(1)} async-done(((s32[2,32,16]{2,0,1:T(2,128)}), s32[2,32,16]{2,0,1:T(2,128)S(1)}, u32[]{:S(2)}, u32[]{:S(2)}) %all-to-all-start) | async-done | bytes 4128 | tf_op jit(solution)/shard_map/all_to_all | solution.py:47
  32.4 0.1 eq.74
  32.5 0.0 copy-start.1
  32.5 18.0 %fusion = f32[2,512,128]{2,1,0:T(8,128)S(1)} fusion(f32[2,8192,128]{2,1,0:T(8,128)} %param.5, s32[2,512]{1,0:T(2,128)S(1)} %eq.74), kind=kOutput, calls=%fused_computation.1 | convolution fusion | flops 12893290496 | bytes 8916992 | tf_op jit(solution)/shard_map/vmap()/while/body/eval_jaxpr/dot_general | solution.py:16
  50.5 0.0 copy-start
  50.5 0.9 copy.25
  51.4 2.6 %all-to-all-start.2 = ((f32[2,32,16,128]{3,2,0,1:T(8,128)}), f32[2,32,16,128]{3,2,0,1:T(8,128)S(1)}, u32[]{:S(2)}, u32[]{:S(2)}) async-start(f32[2,32,16,128]{3,2,0,1:T(8,128)} %copy.25), calls=%async_computation.2 | async-start | bytes 1048576 | tf_op jit(solution)/shard_map/all_to_all | solution.py:53
  54.0 0.2 all-reduce.2.cloned.1.call-start
  54.2 0.0 copy-done.1
  54.3 11.7 %fusion.2 = f32[2,256,128]{2,1,0:T(8,128)} fusion(f32[2,8192,128]{2,1,0:T(8,128)} %param.5, s32[2,256]{1,0:T(2,128)S(1)} %compare_select_fusion.1), kind=kOutput, calls=%fused_computation.4 | convolution fusion | flops 6446645248 | bytes 8652800 | tf_op jit(solution)/shard_map/vmap()/while/body/eval_jaxpr/dot_general | solution.py:16
  66.0 0.0 all-reduce.2.cloned.1.call-update
  66.0 0.0 copy-done
  66.0 0.1 copy.26
  66.2 0.8 convert_reduce_fusion
  67.0 2.6 %all-to-all-done.2 = f32[2,32,16,128]{3,2,0,1:T(8,128)S(1)} async-done(((f32[2,32,16,128]{3,2,0,1:T(8,128)}), f32[2,32,16,128]{3,2,0,1:T(8,128)S(1)}, u32[]{:S(2)}, u32[]{:S(2)}) %all-to-all-start.2) | async-done | bytes 524320 | tf_op jit(solution)/shard_map/all_to_all | solution.py:53
  69.6 1.5 convolution_bitcast_fusion
  71.1 122.8 %all-reduce.2.cloned.1.call-done = f32[2,256,128]{2,1,0:T(8,128)} async-done(((f32[2,256,128]{2,1,0:T(8,128)}), f32[2,256,128]{2,1,0:T(8,128)}) %all-reduce.2.cloned.1.call-update) | async-done | bytes 262160 | tf_op jit(solution)/shard_map/psum | solution.py:35
  194.0 1.6 fusion.4
  195.6 0.8 copy.29
  (3 shorter events, 0.0 us)
Async XLA Ops:
  7.9 14.6 %all-to-all-start.1 = ((s32[2,32,16]{2,0,1:T(2,128)}), s32[2,32,16]{2,0,1:T(2,128)S(1)}, u32[]{:S(2)}, u32[]{:S(2)}) async-start(s32[2,32,16]{2,0,1:T(2,128)} %bitcast.1), calls=%async_computation.1 | async-start | bytes 65536 | tf_op jit(solution)/shard_map/all_to_all | solution.py:46
  22.5 9.8 %all-to-all-start = ((s32[2,32,16]{2,0,1:T(2,128)}), s32[2,32,16]{2,0,1:T(2,128)S(1)}, u32[]{:S(2)}, u32[]{:S(2)}) async-start(s32[2,32,16]{2,0,1:T(2,128)} %bitcast), calls=%async_computation | async-start | bytes 65536 | tf_op jit(solution)/shard_map/all_to_all | solution.py:47
  32.5 21.8 %copy-start.1 = (s32[2,256]{1,0:T(2,128)S(1)}, s32[2,256]{1,0:T(2,128)}, u32[]{:S(2)}) copy-start(s32[2,256]{1,0:T(2,128)} %param.8) | copy-start | bytes 6148
  50.5 15.5 %copy-start = (s32[128,2,8]{0,2,1:T(8,128)S(1)}, s32[128,2,8]{0,2,1:T(8,128)}, u32[]{:S(2)}) copy-start(s32[128,2,8]{0,2,1:T(8,128)} %param.9) | copy-start | bytes 24580
  51.4 18.2 %all-to-all-start.2 = ((f32[2,32,16,128]{3,2,0,1:T(8,128)}), f32[2,32,16,128]{3,2,0,1:T(8,128)S(1)}, u32[]{:S(2)}, u32[]{:S(2)}) async-start(f32[2,32,16,128]{3,2,0,1:T(8,128)} %copy.25), calls=%async_computation.2 | async-start | bytes 1048576 | tf_op jit(solution)/shard_map/all_to_all | solution.py:53
  54.0 140.0 %all-reduce.2.cloned.1.call-start = ((), (), s32[]{:S(2)}) async-start(), calls=%async_computation.3 | async-start | bytes 524288 | tf_op jit(solution)/shard_map/psum | solution.py:35
Sparse Core Ops, SparseCore 0:
  66.1 127.7 all-reduce.1
where the time goes:
time: 204 us; the launch traced here: 203 us
  waiting for transfers between devices  139 us (68%)
  matrix products  32.8 us (16%)
  between operations  13.5 us (7%)
  starting transfers between devices  12.7 us (6%)
  local copies, waits for them, and re-layouts  4.66 us (2%)
    psum x1, waiting for transfers between devices, body(): hot_table = lax.psum(picked, ('gx', 'gy'))  123 us
    dot_general x2, matrix products, one_block(): jnp.dot(selector, table, precision=lax.Precision.HIGHEST, preferred_eleme...  29.7 us
    all_to_all x1, starting transfers between devices, body(): lax.all_to_all(my_rows, ('gx', 'gy'), split_axis=1, concat_axis=1, tiled=...  7.33 us
    all_to_all x1, waiting for transfers between devices, body(): lax.all_to_all(my_bags, ('gx', 'gy'), split_axis=1, concat_axis=1, tiled=...  7.25 us
    all_to_all x1, waiting for transfers between devices, body(): lax.all_to_all(my_rows, ('gx', 'gy'), split_axis=1, concat_axis=1, tiled=...  5.86 us
  transfers between devices with their start and end apart: 4, of which 4 were waited for; matrix products, arithmetic and copies ran while one was open for 8% of the time, Pallas kernels for 0%

commit v1 on v0

--- a/solution.py
+++ b/solution.py
@@ -43,7 +43,15 @@
     my_rows = cold_rows[0]
     my_bags = cold_bags[0]
     got_rows, got_bags = (
-        lax.all_to_all(my_rows, ("gx", "gy"), split_axis=1, concat_axis=1, tiled=True),
+        jnp.concatenate(
+            jax.lax.all_to_all(
+                jnp.stack(jnp.split(my_rows, jax.lax.axis_size(("gx", "gy")), axis=1), axis=0),
+                axis_name=("gx", "gy"),
+                concat_axis=0,
+                split_axis=0,
+            ),
+            axis=1,
+        ),
         lax.all_to_all(my_bags, ("gx", "gy"), split_axis=1, concat_axis=1, tiled=True),
     )
     wanted_rows = jnp.where(got_bags >= 0, got_rows, -1)

time: 204 us -> 225 us (1.10)
  local copies, waits for them, and re-layouts: 4.66 us -> 25.7 us
    unnamed x7 -> x37, local copies, waits for them, and re-layouts: 2.96 us -> 19.3 us
    split x0 -> x2, local copies, waits for them, and re-layouts: none -> 4.08 us  [body(): jnp.split(my_rows, jax.lax.axis_size(('gx', 'gy')), axis=1)]
  transfers between devices with their start and end apart: 4 -> 4, of which waited for: 4 -> 4; matrix products, arithmetic and copies ran while one was open for 8% -> 7% of each run, Pallas kernels for 0% -> 0%
where the time goes in v1:
time: 225 us; the launch traced here: 224 us
  waiting for transfers between devices  139 us (62%)
  matrix products  32.8 us (15%)
  local copies, waits for them, and re-layouts  25.7 us (11%)
  between operations  13.5 us (6%)
  starting transfers between devices  12.7 us (6%)
    psum x1, waiting for transfers between devices, body(): hot_table = lax.psum(picked, ('gx', 'gy'))  123 us
    dot_general x2, matrix products, one_block(): jnp.dot(selector, table, precision=lax.Precision.HIGHEST, preferred_eleme...  29.8 us
    unnamed x37, local copies, waits for them, and re-layouts  19.3 us
    all_to_all x1, starting transfers between devices, body(): jax.lax.all_to_all(jnp.stack(jnp.split(my_rows, jax.lax.axis_size(('gx',...  7.33 us
    all_to_all x1, waiting for transfers between devices, body(): lax.all_to_all(my_bags, ('gx', 'gy'), split_axis=1, concat_axis=1, tiled=...  7.25 us
    all_to_all x1, waiting for transfers between devices, body(): jax.lax.all_to_all(jnp.stack(jnp.split(my_rows, jax.lax.axis_size(('gx',...  5.85 us
  transfers between devices with their start and end apart: 4, of which 4 were waited for; matrix products, arithmetic and copies ran while one was open for 7% of the time, Pallas kernels for 0%

profile of v1, /device:TPU:0, one launch (start us, length us, event | category | flops | bytes accessed | tf_op | source)
XLA Modules:
  0.0 224.3 jit_solution(7283428008566855628)
XLA Ops:
  6.5 1.8 slice_reduce_fusion.19
  8.4 2.3 %slice_reduce_fusion = (s32[2,16]{1,0:T(2,128)S(1)}, s32[2,16]{1,0:T(2,128)S(1)}, s32[2,16]{1,0:T(2,128)S(1)}, s32[2,16]{1,0:T(2,128)S(1)}, s32[2,16]{1,0:T(2,12...) fusion(s32[2,32,16]{1,2,0:T(8,128)} %bitcast.80), kind=kLoop, calls=%fused_computation.47 | loop fusion | bytes 4864 | tf_op jit(solution)/shard_map/split | solution.py:48
  10.6 0.6 constant_dynamic-update-slice_fusion.31
  11.2 0.6 constant_dynamic-update-slice_fusion.30
  11.8 0.6 constant_dynamic-update-slice_fusion.29
  12.4 0.6 constant_dynamic-update-slice_fusion.28
  13.0 0.6 constant_dynamic-update-slice_fusion.27
  13.6 0.6 constant_dynamic-update-slice_fusion.26
  14.1 0.6 constant_dynamic-update-slice_fusion.25
  14.7 0.6 constant_dynamic-update-slice_fusion.24
  15.3 0.6 constant_dynamic-update-slice_fusion.23
  15.8 0.5 constant_dynamic-update-slice_fusion.22
  16.4 0.6 constant_dynamic-update-slice_fusion.21
  17.0 0.6 constant_dynamic-update-slice_fusion.20
  17.6 0.5 constant_dynamic-update-slice_fusion.19
  18.1 0.6 constant_dynamic-update-slice_fusion.18
  18.7 0.6 constant_dynamic-update-slice_fusion.17
  19.3 0.6 constant_dynamic-update-slice_fusion.16
  19.8 0.6 constant_dynamic-update-slice_fusion.15
  20.4 0.6 constant_dynamic-update-slice_fusion.14
  21.0 0.6 constant_dynamic-update-slice_fusion.13
  21.5 0.5 constant_dynamic-update-slice_fusion.12
  22.1 0.6 constant_dynamic-update-slice_fusion.11
  22.7 0.6 constant_dynamic-update-slice_fusion.10
  23.3 0.5 constant_dynamic-update-slice_fusion.9
  23.8 0.6 constant_dynamic-update-slice_fusion.8
  24.4 0.6 constant_dynamic-update-slice_fusion.7
  25.0 0.6 constant_dynamic-update-slice_fusion.6
  25.5 0.6 constant_dynamic-update-slice_fusion.5
  26.1 0.6 constant_dynamic-update-slice_fusion.4
  26.7 0.5 constant_dynamic-update-slice_fusion.3
  27.2 0.6 constant_dynamic-update-slice_fusion.2
  27.8 0.6 constant_dynamic-update-slice_fusion.1
  28.4 0.6 constant_dynamic-update-slice_fusion
  29.0 7.3 %all-to-all-start.1 = ((s32[32,2,1,16]{3,1,2,0:T(2,128)}), s32[32,2,1,16]{3,1,2,0:T(2,128)S(1)}, u32[]{:S(2)}, u32[]{:S(2)}) async-start(s32[32,2,1,16]{3,1,2,0:T(2,128)} %constant_dynamic-update-slice_fusion), calls=%async_computation.1 | async-start | bytes 65536 | tf_op jit(solution)/shard_map/all_to_all | solution.py:47
  36.3 1.4 copy.25
  37.7 5.8 %all-to-all-done.1 = s32[32,2,1,16]{3,1,2,0:T(2,128)S(1)} async-done(((s32[32,2,1,16]{3,1,2,0:T(2,128)}), s32[32,2,1,16]{3,1,2,0:T(2,128)S(1)}, u32[]{:S(2)}, u32[]{:S(2)}) %all-to-all-start.1) | async-done | bytes 4128 | tf_op jit(solution)/shard_map/all_to_all | solution.py:47
  43.6 2.6 %all-to-all-start = ((s32[2,32,16]{2,0,1:T(2,128)}), s32[2,32,16]{2,0,1:T(2,128)S(1)}, u32[]{:S(2)}, u32[]{:S(2)}) async-start(s32[2,32,16]{2,0,1:T(2,128)} %bitcast), calls=%async_computation | async-start | bytes 65536 | tf_op jit(solution)/shard_map/all_to_all | solution.py:55
  46.2 7.2 %all-to-all-done = s32[2,32,16]{2,0,1:T(2,128)S(1)} async-done(((s32[2,32,16]{2,0,1:T(2,128)}), s32[2,32,16]{2,0,1:T(2,128)S(1)}, u32[]{:S(2)}, u32[]{:S(2)}) %all-to-all-start) | async-done | bytes 4128 | tf_op jit(solution)/shard_map/all_to_all | solution.py:55
  53.5 0.1 eq.74
  53.5 0.0 copy-start.1
  53.6 18.0 %fusion = f32[2,512,128]{2,1,0:T(8,128)S(1)} fusion(f32[2,8192,128]{2,1,0:T(8,128)} %param.5, s32[2,512]{1,0:T(2,128)S(1)} %eq.74), kind=kOutput, calls=%fused_computation.1 | convolution fusion | flops 12893290496 | bytes 8916992 | tf_op jit(solution)/shard_map/vmap()/while/body/eval_jaxpr/dot_general | solution.py:16
  71.6 0.0 copy-start
  71.6 0.9 copy.27
  72.5 2.6 %all-to-all-start.2 = ((f32[2,32,16,128]{3,2,0,1:T(8,128)}), f32[2,32,16,128]{3,2,0,1:T(8,128)S(1)}, u32[]{:S(2)}, u32[]{:S(2)}) async-start(f32[2,32,16,128]{3,2,0,1:T(8,128)} %copy.27), calls=%async_computation.2 | async-start | bytes 1048576 | tf_op jit(solution)/shard_map/all_to_all | solution.py:61
  75.1 0.2 all-reduce.2.cloned.1.call-start
  75.3 0.0 copy-done.1
  75.4 11.7 %fusion.2 = f32[2,256,128]{2,1,0:T(8,128)} fusion(f32[2,8192,128]{2,1,0:T(8,128)} %param.5, s32[2,256]{1,0:T(2,128)S(1)} %compare_select_fusion.1), kind=kOutput, calls=%fused_computation.4 | convolution fusion | flops 6446645248 | bytes 8652800 | tf_op jit(solution)/shard_map/vmap()/while/body/eval_jaxpr/dot_general | solution.py:16
  87.1 0.0 all-reduce.2.cloned.1.call-update
  87.1 0.0 copy-done
  87.1 0.1 copy.28
  87.3 0.8 convert_reduce_fusion
  88.1 2.6 %all-to-all-done.2 = f32[2,32,16,128]{3,2,0,1:T(8,128)S(1)} async-done(((f32[2,32,16,128]{3,2,0,1:T(8,128)}), f32[2,32,16,128]{3,2,0,1:T(8,128)S(1)}, u32[]{:S(2)}, u32[]{:S(2)}) %all-to-all-start.2) | async-done | bytes 524320 | tf_op jit(solution)/shard_map/all_to_all | solution.py:61
  90.7 1.5 convolution_bitcast_fusion
  92.2 122.9 %all-reduce.2.cloned.1.call-done = f32[2,256,128]{2,1,0:T(8,128)} async-done(((f32[2,256,128]{2,1,0:T(8,128)}), f32[2,256,128]{2,1,0:T(8,128)}) %all-reduce.2.cloned.1.call-update) | async-done | bytes 262160 | tf_op jit(solution)/shard_map/psum | solution.py:35
  215.1 1.6 fusion.4
  216.7 0.8 copy.31
  (3 shorter events, 0.0 us)
Async XLA Ops:
  29.0 14.6 %all-to-all-start.1 = ((s32[32,2,1,16]{3,1,2,0:T(2,128)}), s32[32,2,1,16]{3,1,2,0:T(2,128)S(1)}, u32[]{:S(2)}, u32[]{:S(2)}) async-start(s32[32,2,1,16]{3,1,2,0:T(2,128)} %constant_dynamic-update-slice_fusion), calls=%async_computation.1 | async-start | bytes 65536 | tf_op jit(solution)/shard_map/all_to_all | solution.py:47
  43.6 9.8 %all-to-all-start = ((s32[2,32,16]{2,0,1:T(2,128)}), s32[2,32,16]{2,0,1:T(2,128)S(1)}, u32[]{:S(2)}, u32[]{:S(2)}) async-start(s32[2,32,16]{2,0,1:T(2,128)} %bitcast), calls=%async_computation | async-start | bytes 65536 | tf_op jit(solution)/shard_map/all_to_all | solution.py:55
  53.5 21.8 %copy-start.1 = (s32[2,256]{1,0:T(2,128)S(1)}, s32[2,256]{1,0:T(2,128)}, u32[]{:S(2)}) copy-start(s32[2,256]{1,0:T(2,128)} %param.8) | copy-start | bytes 6148
  71.6 15.5 %copy-start = (s32[128,2,8]{0,2,1:T(8,128)S(1)}, s32[128,2,8]{0,2,1:T(8,128)}, u32[]{:S(2)}) copy-start(s32[128,2,8]{0,2,1:T(8,128)} %param.9) | copy-start | bytes 24580
  72.5 18.2 %all-to-all-start.2 = ((f32[2,32,16,128]{3,2,0,1:T(8,128)}), f32[2,32,16,128]{3,2,0,1:T(8,128)S(1)}, u32[]{:S(2)}, u32[]{:S(2)}) async-start(f32[2,32,16,128]{3,2,0,1:T(8,128)} %copy.27), calls=%async_computation.2 | async-start | bytes 1048576 | tf_op jit(solution)/shard_map/all_to_all | solution.py:61
  75.1 140.0 %all-reduce.2.cloned.1.call-start = ((), (), s32[]{:S(2)}) async-start(), calls=%async_computation.3 | async-start | bytes 524288 | tf_op jit(solution)/shard_map/psum | solution.py:35
Sparse Core Ops, SparseCore 0:
  87.2 127.8 all-reduce.1
